TPU v7x, 16 devices: a whole 2x2x2 slice. The times are simulated.
16 devices in a mesh: fsdp: 16 (over z, y, x, core).
Axes of the slice: x: 2, y: 2, z: 2, core: 2. Of those that a mesh axis runs over, the one named last changes fastest.
Arguments:
- token_ids: int32 [512, 512], P('fsdp')
- embed_table: bfloat16 [49152, 960], P('fsdp')
- norm_gain: bfloat16 [960], P('fsdp')
- w_query: bfloat16 [960, 15, 64], P('fsdp')
- w_key: bfloat16 [960, 5, 64], P('fsdp')
- w_value: bfloat16 [960, 5, 64], P('fsdp')
- w_out: bfloat16 [960, 960], P('fsdp')
- grad_out: bfloat16 [512, 512, 960], P('fsdp')
Outputs:
- output 1: bfloat16 [512, 512, 960], P('fsdp')
- output 2: float32 [49152, 960], P('fsdp')
- output 3: float32 [960], P('fsdp')
- output 4: float32 [960, 15, 64], P('fsdp')
- output 5: float32 [960, 5, 64], P('fsdp')
- output 6: float32 [960, 5, 64], P('fsdp')
- output 7: float32 [960, 960], P('fsdp')
All inputs are finite; a program needn't handle non-finite values.
Results may differ from a plain program's by a relative error of at most 0.00861237.
Values are sent between devices in bfloat16 or wider.
A program may use at most 1 GiB of HBM per device.

v0:
```python
import jax
import jax.numpy as jnp
from jax import lax
from jax.sharding import PartitionSpec as P

ROPE_THETA = 500000.0
NORM_EPS = 1e-5
CHUNK_COUNT = 4


def rms_scale(values):
    return values * lax.rsqrt(jnp.mean(values * values, axis=-1, keepdims=True) + NORM_EPS)


def input_norm(x_float, gain):
    return rms_scale(x_float) * gain


def rotary_norm(values):
    seq_len = values.shape[1]
    half = values.shape[-1] // 2
    frequency = ROPE_THETA ** (-2.0 * jnp.arange(half, dtype=jnp.float32) / values.shape[-1])
    angles = jnp.arange(seq_len, dtype=jnp.float32)[:, None] * frequency[None, :]
    cosine = jnp.cos(angles)[:, None, :]
    sine = jnp.sin(angles)[:, None, :]
    first = values[..., :half]
    second = values[..., half:]
    rotated = jnp.concatenate([first * cosine - second * sine, second * cosine + first * sine], axis=-1)
    return rms_scale(rotated)


def block_forward(embedded, gain, w_query, w_key, w_value, w_out):
    batch, seq_len, d_model = embedded.shape
    heads, head_dim = w_query.shape[1], w_query.shape[2]
    kv_heads = w_key.shape[1]
    group = heads // kv_heads
    chunk = seq_len // CHUNK_COUNT
    x_float = embedded.astype(jnp.float32)
    normed_f, norm_pull = jax.vjp(input_norm, x_float, gain.astype(jnp.float32))
    normed = normed_f.astype(jnp.bfloat16)
    q_raw = jnp.einsum('bsd,dhe->bshe', normed, w_query, preferred_element_type=jnp.float32)
    k_raw = jnp.einsum('bsd,dhe->bshe', normed, w_key, preferred_element_type=jnp.float32)
    value_bf = jnp.einsum('bsd,dhe->bshe', normed, w_value, preferred_element_type=jnp.float32).astype(jnp.bfloat16)
    q_norm, q_pull = jax.vjp(rotary_norm, q_raw)
    k_norm, k_pull = jax.vjp(rotary_norm, k_raw)
    query_bf = q_norm.astype(jnp.bfloat16).reshape(batch, CHUNK_COUNT, chunk, kv_heads, group, head_dim)
    key_bf = k_norm.astype(jnp.bfloat16).reshape(batch, CHUNK_COUNT, chunk, kv_heads, head_dim)
    value_bf = value_bf.reshape(batch, CHUNK_COUNT, chunk, kv_heads, head_dim)
    scores = jnp.einsum('bcikgd,bcjkd->bckigj', query_bf, key_bf, preferred_element_type=jnp.float32) * head_dim ** -0.5
    causal = jnp.arange(chunk)[:, None, None] >= jnp.arange(chunk)[None, None, :]
    attn_probs = jax.nn.softmax(jnp.where(causal, scores, -1e30), axis=-1)
    probs_bf = attn_probs.astype(jnp.bfloat16)
    mixed_bf = jnp.einsum('bckigj,bcjkd->bcikgd', probs_bf, value_bf, preferred_element_type=jnp.float32).astype(jnp.bfloat16).reshape(batch, seq_len, heads * head_dim)
    hidden = (x_float + jnp.einsum('bsq,qd->bsd', mixed_bf, w_out, preferred_element_type=jnp.float32)).astype(jnp.bfloat16)
    saved = dict(normed=normed, norm_pull=norm_pull, q_pull=q_pull, k_pull=k_pull, query_bf=query_bf, key_bf=key_bf, value_bf=value_bf, attn_probs=attn_probs, probs_bf=probs_bf, mixed_bf=mixed_bf)
    return hidden, saved


def block_backward(grad_out, saved, w_query, w_key, w_value, w_out):
    batch, seq_len, d_model = grad_out.shape
    heads, head_dim = w_query.shape[1], w_query.shape[2]
    kv_heads = w_key.shape[1]
    group = heads // kv_heads
    chunk = seq_len // CHUNK_COUNT
    attn_probs = saved['attn_probs']
    normed = saved['normed']
    grad_wout = jnp.einsum('bsq,bsd->qd', saved['mixed_bf'], grad_out, preferred_element_type=jnp.float32)
    d_mixed = jnp.einsum('bsd,qd->bsq', grad_out, w_out, preferred_element_type=jnp.float32).astype(jnp.bfloat16).reshape(batch, CHUNK_COUNT, chunk, kv_heads, group, head_dim)
    d_probs = jnp.einsum('bcikgd,bcjkd->bckigj', d_mixed, saved['value_bf'], preferred_element_type=jnp.float32)
    d_value = jnp.einsum('bckigj,bcikgd->bcjkd', saved['probs_bf'], d_mixed, preferred_element_type=jnp.float32)
    d_scores = attn_probs * (d_probs - jnp.sum(attn_probs * d_probs, axis=-1, keepdims=True)) * head_dim ** -0.5
    dscore_bf = d_scores.astype(jnp.bfloat16)
    d_query = jnp.einsum('bckigj,bcjkd->bcikgd', dscore_bf, saved['key_bf'], preferred_element_type=jnp.float32).reshape(batch, seq_len, heads, head_dim)
    d_key = jnp.einsum('bckigj,bcikgd->bcjkd', dscore_bf, saved['query_bf'], preferred_element_type=jnp.float32).reshape(batch, seq_len, kv_heads, head_dim)
    dq_raw = saved['q_pull'](d_query)[0].astype(jnp.bfloat16)
    dk_raw = saved['k_pull'](d_key)[0].astype(jnp.bfloat16)
    dv_raw = d_value.reshape(batch, seq_len, kv_heads, head_dim).astype(jnp.bfloat16)
    grad_query = jnp.einsum('bsd,bshe->dhe', normed, dq_raw, preferred_element_type=jnp.float32)
    grad_key = jnp.einsum('bsd,bshe->dhe', normed, dk_raw, preferred_element_type=jnp.float32)
    grad_value = jnp.einsum('bsd,bshe->dhe', normed, dv_raw, preferred_element_type=jnp.float32)
    d_normed = (jnp.einsum('bshe,dhe->bsd', dq_raw, w_query, preferred_element_type=jnp.float32)
                + jnp.einsum('bshe,dhe->bsd', dk_raw, w_key, preferred_element_type=jnp.float32)
                + jnp.einsum('bshe,dhe->bsd', dv_raw, w_value, preferred_element_type=jnp.float32))
    dx_norm, grad_gain = saved['norm_pull'](d_normed)
    d_embedded = grad_out.astype(jnp.float32) + dx_norm
    return d_embedded, grad_gain, grad_query, grad_key, grad_value, grad_wout


def solution(mesh):
    group_count = mesh.shape['fsdp']

    def reduce_share(full_grad):
        return lax.psum_scatter(full_grad, 'fsdp', scatter_dimension=0, tiled=True) / group_count

    def device_step(token_ids, embed_table, norm_gain, w_query, w_key, w_value, w_out, grad_out):
        full_table = lax.all_gather(embed_table, 'fsdp', axis=0, tiled=True)
        gain_full = lax.all_gather(norm_gain, 'fsdp', axis=0, tiled=True)
        query_full = lax.all_gather(w_query, 'fsdp', axis=0, tiled=True)
        key_full = lax.all_gather(w_key, 'fsdp', axis=0, tiled=True)
        value_full = lax.all_gather(w_value, 'fsdp', axis=0, tiled=True)
        wout_full = lax.all_gather(w_out, 'fsdp', axis=0, tiled=True)
        embedded = jnp.take(full_table, token_ids, axis=0)
        hidden, saved = block_forward(embedded, gain_full, query_full, key_full, value_full, wout_full)
        d_embedded, grad_gain, grad_query, grad_key, grad_value, grad_wout = block_backward(grad_out, saved, query_full, key_full, value_full, wout_full)
        table_grad = jax.ops.segment_sum(d_embedded.reshape(-1, d_embedded.shape[-1]), token_ids.reshape(-1), num_segments=full_table.shape[0])
        return (hidden, reduce_share(table_grad), reduce_share(grad_gain), reduce_share(grad_query), reduce_share(grad_key), reduce_share(grad_value), reduce_share(grad_wout))

    tokens = P('fsdp', None, None)
    matrix = P('fsdp', None)
    vector = P('fsdp')
    return jax.shard_map(device_step, mesh=mesh, in_specs=(matrix, matrix, vector, tokens, tokens, tokens, matrix, tokens), out_specs=(tokens, matrix, vector, tokens, tokens, tokens, matrix), check_vma=False)
```

profile of v0, /device:TPU:0, one launch (start us, length us, event | category | flops | bytes accessed | tf_op | source)
XLA Modules:
  0.0 3807.5 jit_solution(17823507195355022642)
XLA Ops:
  198.1 236.0 %all-gather.5.cloned.1.call-done = bf16[49152,960]{1,0:T(8,128)(2,1)} async-done(((bf16[3072,960]{1,0:T(8,128)(2,1)}), bf16[49152,960]{1,0:T(8,128)(2,1)}) %all-gather.5.cloned.1.call-update) | async-done | bytes 94371856 | tf_op jit(solution)/shard_map/all_gather | solution.py:96
  434.1 299.6 %gather_fusion = bf16[16384,960]{1,0:T(8,128)(2,1)} fusion(bf16[49152,960]{1,0:T(8,128)(2,1)} %all-gather.5.cloned.1.call-done, s32[16384]{0:T(1024)S(1)} %broadcast_clamp_fusion.1), kind=kCustom, calls=%fused_computation | custom fusion | bytes 62980096 | tf_op jit(solution)/shard_map/jit(_take)/gather | solution.py:102
  733.7 43.7 %copy.128 = bf16[32,512,960]{1,2,0:T(8,128)(2,1)} copy(bf16[32,512,960]{2,1,0:T(8,128)(2,1)} %bitcast.186) | data formatting | bytes 62914560 | tf_op jit(solution)/shard_map/jit(_take)/gather | solution.py:102
  792.5 44.6 %fusion.64 = f32[32,512,15,64]{1,3,2,0:T(8,128)} fusion(bf16[960,15,64]{0,2,1:T(8,128)(2,1)S(1)} %copy.131, f32[960]{0:T(1024)S(1)} %copy-done.34, f32[32,512]{1,0:T(8,128)S(1)} %fusion.84, bf16[32,512,960]{1,2,0:T(8,128)(2,1)} %copy.128, pred[32,512]{1,0:T(8,128)(4,1)S(1)} %copy-done.30), kind=kOutput, calls=%fused_computation.94 | convolution fusion | flops 30277632000 | bytes 96300800 | tf_op jit(solution)/shard_map/bsd,dhe->bshe/dot_general | solution.py:41
  1126.1 71.0 %fusion.44 = f32[32,4,5,128,3,128]{3,5,4,2,1,0:T(8,128)} fusion(f32[32,4,128,5,3,64]{2,5,4,3,1,0:T(8,128)} %copy_dynamic-update-slice_fusion, f32[32,4,128,5,3]{2,4,3,1,0:T(4,128)S(1)} %copy.135, f32[32,4,128,5,64]{2,4,3,1,0:T(8,128)} %bitcast_dynamic-update-slice_fusion, f32[32,4,128,5]{2,3,1,0:T(8,128)S(1)} %copy.141), kind=kOutput, calls=%fused_computation.69 | convolution fusion | flops 4068474880 | bytes 211025920 | tf_op jit(solution)/shard_map/bcikgd,bcjkd->bckigj/dot_general | solution.py:49
  1197.1 121.3 %fusion.102 = (f32[32,4,5,128,3]{3,4,2,1,0:T(4,128)S(1)}, f32[32,4,5,128,3,128]{3,5,4,2,1,0:T(8,128)}) fusion(f32[32,4,5,128,3,128]{3,5,4,2,1,0:T(8,128)} %fusion.44, pred[128,128]{0,1:T(8,128)(4,1)S(1)} %copy-done.37), kind=kOutput, calls=%fused_computation.141 | output fusion | flops 188743808 | bytes 252657664 | tf_op jit(solution)/shard_map/sub | solution.py:51
  1318.4 57.2 %fusion.36 = f32[32,4,5,128,3,128]{3,5,4,2,1,0:T(8,128)} fusion(bf16[32,4,128,5,3,64]{2,1,5,4,3,0:T(4,128)(2,1)} %reshape.181, bf16[32,4,128,5,64,1]{2,1,4,3,0,5:T(4,128)(2,1)} %bitcast.187), kind=kOutput, calls=%fused_computation.57 | convolution fusion | flops 4026531840 | bytes 167772160 | tf_op jit(solution)/shard_map/bcikgd,bcjkd->bckigj/dot_general | solution.py:69
  1375.6 179.8 %fusion.41 = (f32[32,4,128,5]{2,3,1,0:T(8,128)}, f32[32,4,5,64,128,1]{4,3,5,2,1,0:T(8,128)}) fusion(f32[32,4,128,5,64]{2,4,3,1,0:T(8,128)} %bitcast_dynamic-update-slice_fusion, f32[32,4,5,128,3,128]{3,5,4,2,1,0:T(8,128)} %fusion.36, f32[32,4,5,128,3,128]{3,5,4,2,1,0:T(8,128)} %get-tuple-element.53, f32[32,4,5,128,3]{3,4,2,1,0:T(4,128)S(1)} %get-tuple-element.52, ...), kind=kOutput, calls=%fused_computation.64 | convolution fusion | flops 4288839680 | bytes 358809600 | tf_op jit(solution)/shard_map/bckigj,bcikgd->bcjkd/dot_general | solution.py:74
  1555.4 195.3 %multiply_reduce_fusion.1 = (f32[32,4,128,5,3]{2,4,3,1,0:T(4,128)}, f32[32,4,128,5,3,64]{2,5,4,3,1,0:T(8,128)}) fusion(f32[32,4,128,5,3,64]{2,5,4,3,1,0:T(8,128)} %copy_dynamic-update-slice_fusion, f32[32,4,5,128,3,128]{3,5,4,2,1,0:T(8,128)} %fusion.36, f32[32,4,5,128,3,128]{3,5,4,2,1,0:T(8,128)} %get-tuple-element.53, ...), kind=kOutput, calls=%fused_computation.33 | convolution fusion | flops 4288675840 | bytes 400752640 | tf_op jit(solution)/shard_map/bckigj,bcjkd->bcikgd/dot_general | solution.py:73
  1750.7 59.9 %fusion.46 = bf16[32,4,5,8,8,128]{5,4,3,2,1,0:T(8,128)(2,1)} fusion(bf16[32,4,128,5,3,64]{2,1,5,4,3,0:T(4,128)(2,1)} %reshape.181, f32[32,4,5,128,3,128]{3,5,4,2,1,0:T(8,128)} %get-tuple-element.53, f32[32,4,5,128,3]{3,4,2,1,0:T(4,128)} %copy-done.39), kind=kOutput, calls=%fused_computation.71 | convolution fusion | flops 4094689280 | bytes 168755200 | tf_op jit(solution)/shard_map/bckigj,bcikgd->bcjkd/dot_general | solution.py:70
  1899.9 69.8 %copy.149 = f32[32,4,128,5,3,64]{2,1,5,4,3,0:T(4,128)} copy(f32[32,4,128,5,3,64]{2,5,4,3,1,0:T(8,128)} %get-tuple-element.57) | data formatting | bytes 125829120 | tf_op jit(solution)/shard_map/bckigj,bcjkd->bcikgd/transpose | solution.py:73
  1969.7 73.0 %reshape.182 = f32[32,512,15,64]{1,3,2,0:T(8,128)} reshape(f32[32,4,128,5,3,64]{2,1,5,4,3,0:T(4,128)} %copy.149) | data formatting | bytes 125829120 | tf_op jit(solution)/shard_map/reshape | solution.py:73
  2042.7 67.3 %add_add_fusion.1 = f32[32,512,15,64]{1,3,2,0:T(8,128)} fusion(f32[32,512,15,64]{1,3,2,0:T(8,128)} %reshape.182, f32[32,512,15,32]{1,3,2,0:T(8,128)} %get-tuple-element.44, f32[32,512,15,32]{1,3,2,0:T(8,128)} %get-tuple-element.45, f32[32,512,15]{1,2,0:T(8,128)S(1)} %multiply_multiply_fusion, f32[32,512,15]{1,2,0:T(8,128)S(1)} %copy-done.4), kind=kLoop, calls=%fused_computation.19 | loop fusion | flops 78643200 | bytes 190709760 | tf_op jit(solution)/shard_map/transpose(jvp())/add_any | solution.py:12
  2181.9 74.4 %fusion.62 = f32[960,15,64]{2,0,1:T(8,128)} fusion(f32[32,512,15,32]{1,3,2,0:T(8,128)} %get-tuple-element.43, f32[32,512,15,32]{1,3,2,0:T(8,128)} %get-tuple-element.42, f32[960]{0:T(1024)S(1)} %copy-done.36, f32[32,512]{1,0:T(8,128)S(1)} %copy-done.29, bf16[32,512,960]{1,2,0:T(8,128)(2,1)} %copy.128, pred[32,512]{1,0:T(8,128)(4,1)S(1)} %copy-done.32), kind=kOutput, calls=%fused_computation.91 | convolution fusion | flops 30309089280 | bytes 98144000 | tf_op jit(solution)/shard_map/bsd,bshe->dhe/dot_general | solution.py:78
  2256.3 53.5 %fusion.59 = f32[32,512,960,1]{1,2,3,0:T(8,128)} fusion(f32[32,512,15,32]{1,3,2,0:T(8,128)} %get-tuple-element.43, f32[32,512,15,32]{1,3,2,0:T(8,128)} %get-tuple-element.42, bf16[960,15,64]{2,1,0:T(8,128)(2,1)} %all-gather.7.cloned.1.call-done), kind=kOutput, calls=%fused_computation.88 | convolution fusion | flops 30230446080 | bytes 127672320 | tf_op jit(solution)/shard_map/bshe,dhe->bsd/dot_general | solution.py:81
  2309.8 76.9 %fusion.16 = (f32[960]{0:T(1024)}, f32[32,512]{1,0:T(8,128)S(1)}, f32[32,512,960]{1,2,0:T(8,128)}) fusion(f32[32,512]{1,0:T(8,128)S(1)} %copy-done.29, bf16[32,512,960]{1,2,0:T(8,128)(2,1)} %copy.128, pred[32,512]{1,0:T(8,128)(4,1)S(1)} %copy-done.32, f32[960]{0:T(1024)S(1)} %copy-done.36, bf16[32,4,5,8,8,128]{5,4,3,2,1,0:T(8,128)(2,1)} %fusion.46, ...), kind=kOutput, calls=%fused_computation.24 | convolution fusion | flops 10223598592 | bytes 231456256 | tf_op jit(solution)/shard_map/bshe,dhe->bsd/dot_general | solution.py:83
  2386.7 61.8 %fusion.17 = f32[32,512,960]{1,2,0:T(8,128)} fusion(bf16[32,512,960]{1,2,0:T(8,128)(2,1)} %param.15, f32[32,512,960]{1,2,0:T(8,128)} %get-tuple-element.58, f32[32,512]{1,0:T(8,128)S(1)} %multiply_multiply_fusion.2, f32[960]{0:T(1024)S(1)} %copy-done.36, f32[32,512]{1,0:T(8,128)S(1)} %copy-done.29, bf16[32,512,960]{1,2,0:T(8,128)(2,1)} %copy.128, ...), kind=kLoop, calls=%fused_computation.25 | loop fusion | flops 141557760 | bytes 188894976 | tf_op jit(solution)/shard_map/add | solution.py:85
  2448.5 65.1 %copy.197 = f32[32,512,960]{2,1,0:T(8,128)} copy(f32[32,512,960]{1,2,0:T(8,128)} %fusion.17) | data formatting | bytes 125829120 | tf_op jit(solution)/shard_map/reshape | solution.py:105
  2513.6 361.7 %scatter_custom_fusion = f32[49152,960]{1,0:T(8,128)} fusion(s32[16384]{0:T(1024)} %get-tuple-element.35, f32[]{:T(128)} %constant.24.clone.1, f32[16384,960]{1,0:T(8,128)} %bitcast.32, s32[16384]{0:T(1024)} %broadcast_clamp_fusion), kind=kCustom, calls=%fused_computation.15 | custom fusion | flops 15728640 | bytes 188744192 | tf_op jit(solution)/shard_map/scatter-add | solution.py:105
  2878.7 54.2 %convert_bitcast_fusion = bf16[32,4,128,5,3,64]{2,5,4,3,1,0:T(8,128)(2,1)} fusion(bf16[32,4,128,5,64,1]{2,1,4,3,0,5:T(4,128)(2,1)} %bitcast.188, f32[32,4,5,128,3,128]{3,5,4,2,1,0:T(8,128)} %get-tuple-element.53, f32[32,4,5,128,3]{3,4,2,1,0:T(4,128)S(1)} %copy-done.40), kind=kOutput, calls=%fused_computation.48 | convolution fusion | flops 4105175040 | bytes 168755200 | tf_op jit(solution)/shard_map/bckigj,bcjkd->bcikgd/dot_general | solution.py:53
  2972.8 45.5 %reshape.180 = bf16[32,512,960]{1,2,0:T(8,128)(2,1)} reshape(bf16[32,4,128,5,3,64]{2,1,5,4,3,0:T(4,128)(2,1)} %copy.144) | data formatting | bytes 62914560 | tf_op jit(solution)/shard_map/reshape | solution.py:53
  3059.1 51.5 %fusion.1 = f32[64,960]{1,0:T(8,128)S(1)} fusion(f32[960,960]{1,0:T(8,128)} %convolution_bitcast_fusion), kind=kCustom, calls=%all-reduce-scatter | all-reduce-scatter fusion | flops 983041 | bytes 3932160
  3112.2 45.3 %fusion.19 = bf16[32,512,960]{1,2,0:T(8,128)(2,1)} fusion(bf16[32,512,960]{1,2,0:T(8,128)(2,1)} %reshape.180, bf16[32,512,960]{1,2,0:T(8,128)(2,1)} %copy.128, pred[32,512]{1,0:T(8,128)(4,1)S(1)} %copy-done.33, bf16[960,960]{1,0:T(8,128)(2,1)S(1)} %copy-done.15), kind=kOutput, calls=%fused_computation.27 | convolution fusion | flops 30261903360 | bytes 96231424 | tf_op jit(solution)/shard_map/bsq,qd->bsd/dot_general | solution.py:54
  3196.6 579.6 %reduce-scatter.9.cloned.1.call-done = f32[3072,960]{1,0:T(8,128)} async-done(((f32[49152,960]{1,0:T(8,128)}), f32[3072,960]{1,0:T(8,128)}) %reduce-scatter.9.cloned.1.call-update) | async-done | bytes 11796496
  (179 shorter events, 805.1 us)
Async XLA Ops:
  7.2 98.5 %all-gather.9.cloned.1.call-start = ((), (), s32[]{:S(2)}) async-start(), calls=%async_computation.3 | async-start | bytes 2228224 | tf_op jit(solution)/shard_map/all_gather | solution.py:101
  7.9 185.5 %all-gather.7.cloned.1.call-start = ((), (), s32[]{:S(2)}) async-start(), calls=%async_computation.2 | async-start | bytes 4177920 | tf_op jit(solution)/shard_map/all_gather | solution.py:98
  8.7 425.4 %all-gather.5.cloned.1.call-start = ((), (), s32[]{:S(2)}) async-start(), calls=%async_computation.1 | async-start | bytes 106954752 | tf_op jit(solution)/shard_map/all_gather | solution.py:96
  17.2 3175.4 %all-reduce.15.cloned.1.call-start = ((), (), s32[]{:S(2)}) async-start(), calls=%async_computation.5 | async-start | bytes 24576000
  91.1 58.9 %copy-start.6 = (bf16[960,5,64]{2,1,0:T(8,128)(2,1)}, bf16[960,5,64]{2,1,0:T(8,128)(2,1)S(1)}, u32[]{:S(2)}) copy-start(bf16[960,5,64]{2,1,0:T(8,128)(2,1)S(1)} %all_gather.20) | copy-start | bytes 1843204
  792.4 273.5 %copy-start.27 = (f32[32,512]{1,0:T(8,128)}, f32[32,512]{1,0:T(8,128)S(1)}, u32[]{:S(2)}) copy-start(f32[32,512]{1,0:T(8,128)S(1)} %fusion.84) | copy-start | bytes 196612
  933.8 96.6 %copy-start.1 = (f32[32,512,15]{1,2,0:T(8,128)}, f32[32,512,15]{1,2,0:T(8,128)S(1)}, u32[]{:S(2)}) copy-start(f32[32,512,15]{1,2,0:T(8,128)S(1)} %multiply_reduce_fusion.2) | copy-start | bytes 2949124
  1032.4 93.7 %copy-start.13 = (f32[32,4,128,5]{2,3,1,0:T(8,128)}, f32[32,4,128,5]{2,3,1,0:T(8,128)S(1)}, u32[]{:S(2)}) copy-start(f32[32,4,128,5]{2,3,1,0:T(8,128)S(1)} %copy.141) | copy-start | bytes 983044
  1126.1 71.0 %copy-start.37 = (pred[128,128]{0,1:T(8,128)(4,1)S(1)}, pred[128,128]{0,1:T(8,128)(4,1)}, u32[]{:S(2)}) copy-start(pred[128,128]{0,1:T(8,128)(4,1)} %iota_compare_fusion) | copy-start | bytes 49156
  1318.4 237.0 %copy-start.39 = (f32[32,4,5,128,3]{3,4,2,1,0:T(4,128)}, f32[32,4,5,128,3]{3,4,2,1,0:T(4,128)S(1)}, u32[]{:S(2)}) copy-start(f32[32,4,5,128,3]{3,4,2,1,0:T(4,128)S(1)} %get-tuple-element.52) | copy-start | bytes 2949124
  1375.6 179.8 %copy-start.14 = (f32[32,4,128,5]{2,3,1,0:T(8,128)S(1)}, f32[32,4,128,5]{2,3,1,0:T(8,128)}, u32[]{:S(2)}) copy-start(f32[32,4,128,5]{2,3,1,0:T(8,128)} %copy-done.13) | copy-start | bytes 983044
  1750.7 59.9 %copy-start.26 = (f32[32,4,128,5]{2,3,1,0:T(8,128)S(1)}, f32[32,4,128,5]{2,3,1,0:T(8,128)}, u32[]{:S(2)}) copy-start(f32[32,4,128,5]{2,3,1,0:T(8,128)} %get-tuple-element.54) | copy-start | bytes 983044
  1750.7 60.1 %copy-start.11 = (f32[32,512,5]{1,2,0:T(8,128)S(1)}, f32[32,512,5]{1,2,0:T(8,128)}, u32[]{:S(2)}) copy-start(f32[32,512,5]{1,2,0:T(8,128)} %copy-done.10) | copy-start | bytes 983044
  1750.7 60.6 %copy-start.12 = (f32[32,512,5]{1,2,0:T(8,128)S(1)}, f32[32,512,5]{1,2,0:T(8,128)}, u32[]{:S(2)}) copy-start(f32[32,512,5]{1,2,0:T(8,128)} %copy.155) | copy-start | bytes 983044
  1969.7 73.0 %copy-start.4 = (f32[32,512,15]{1,2,0:T(8,128)S(1)}, f32[32,512,15]{1,2,0:T(8,128)}, u32[]{:S(2)}) copy-start(f32[32,512,15]{1,2,0:T(8,128)} %copy-done.3) | copy-start | bytes 2949124
  2042.6 67.3 %copy-start.18 = (f32[512,32]{0,1:T(8,128)S(1)}, f32[512,32]{0,1:T(8,128)}, u32[]{:S(2)}) copy-start(f32[512,32]{0,1:T(8,128)} %get-tuple-element.50) | copy-start | bytes 196612
  2042.6 67.3 %copy-start.21 = (f32[512,32]{0,1:T(8,128)S(1)}, f32[512,32]{0,1:T(8,128)}, u32[]{:S(2)}) copy-start(f32[512,32]{0,1:T(8,128)} %get-tuple-element.51) | copy-start | bytes 196612
  2042.6 108.3 %slice-start = ((s8[10485760]{0:T(1024)(128)(4,1)}), s8[4194304]{0:T(1024)(128)(4,1)S(1)}, s32[]{:S(2)}) async-start(s8[10485760]{0:T(1024)(128)(4,1)} %bitcast.193), calls=%async_computation.6 | async-start | bytes 8388608
  2042.6 108.3 %slice-start.1 = ((s8[10485760]{0:T(1024)(128)(4,1)}), s8[4194304]{0:T(1024)(128)(4,1)S(1)}, s32[]{:S(2)}) async-start(s8[10485760]{0:T(1024)(128)(4,1)} %bitcast.193), calls=%async_computation.7 | async-start | bytes 8388608
  2309.7 76.9 %copy-start.25 = (f32[32,512]{1,0:T(8,128)S(1)}, f32[32,512]{1,0:T(8,128)}, u32[]{:S(2)}) copy-start(f32[32,512]{1,0:T(8,128)} %copy-done.24) | copy-start | bytes 196612
  2386.7 1389.5 %reduce-scatter.9.cloned.1.call-start = ((), (), s32[]{:S(2)}) async-start(), calls=%async_computation.4 | async-start | bytes 213909504
  3018.3 93.9 %copy-start.15 = (bf16[960,960]{1,0:T(8,128)(2,1)S(1)}, bf16[960,960]{1,0:T(8,128)(2,1)}, u32[]{:S(2)}) copy-start(bf16[960,960]{1,0:T(8,128)(2,1)} %reshape.207) | copy-start | bytes 5529604
  3018.3 93.9 %copy-start.33 = (pred[32,512]{1,0:T(8,128)(4,1)S(1)}, pred[32,512]{1,0:T(8,128)(4,1)}, u32[]{:S(2)}) copy-start(pred[32,512]{1,0:T(8,128)(4,1)} %compare_and_fusion) | copy-start | bytes 49156
  3110.6 81.0 %collective-permute-start = (f32[60,960]{1,0:T(8,128)S(1)}, f32[60,960]{1,0:T(8,128)S(1)}, u32[]{:S(2)}, u32[]{:S(2)}) collective-permute-start(f32[60,960]{1,0:T(8,128)S(1)} %slice.24), channel_id=1, source_target_pairs={{0,1},{1,2},{2,3},{3,4},{4,5},{5,6},{6,7},{7,8},{8,9},{9,10},{10,1... | collective-permute-start | bytes 691208
  (26 other events, 648.4 us)
Sparse Core Ops, SparseCore 0:
  10.2 31.3 all-gather.8
  43.8 36.0 all-gather.6
  82.8 351.2 all-gather.4
  2386.8 143.4 all-reduce.14
  2875.4 900.6 reduce-scatter.8
where the time goes:
time: 3830 us; the launch traced here: 3810 us
  matrix products  1130 us (30%)
  local copies, waits for them, and re-layouts  887 us (23%)
  waiting for transfers between devices  817 us (21%)
  other arithmetic  802 us (21%)
  blocking collectives  152 us (4%)
    unnamed x8, waiting for transfers between devices  581 us
    scatter-add x3, other arithmetic, device_step(): jax.ops.segment_sum(d_embedded.reshape(-1, d_embedded.shape[-1]), token_i...  370 us
    gather x2, local copies, waits for them, and re-layouts, device_step(): embedded = jnp.take(full_table, token_ids, axis=0)  343 us
    all_gather x1, waiting for transfers between devices, device_step(): full_table = lax.all_gather(embed_table, 'fsdp', axis=0, tiled=True)  236 us
    dot_general x1, matrix products, block_backward(): jnp.einsum('bckigj,bcjkd->bcikgd', dscore_bf, saved['key_bf'], preferred_...  195 us
    dot_general x1, matrix products, block_backward(): jnp.einsum('bckigj,bcikgd->bcjkd', dscore_bf, saved['query_bf'], preferre...  180 us
    sub x1, other arithmetic, block_forward(): attn_probs = jax.nn.softmax(jnp.where(causal, scores, -1e+30), axis=-1)  121 us
    unnamed x3, blocking collectives  120 us
  transfers between devices with their start and end apart: 6, of which 2 were waited for; matrix products, arithmetic and copies ran while one was open for 24% of the time, Pallas kernels for 0%

commit v1 on v0

v1 whole, which is shorter than its diff:
```python
import functools

import jax
import jax.numpy as jnp
from jax import lax
from jax.experimental import pallas as pl
from jax.experimental.pallas import tpu as pltpu
from jax.sharding import PartitionSpec as P

ROPE_THETA = 500000.0
NORM_EPS = 1e-5
CHUNK_COUNT = 4
LOG2_E = 1.4426950408889634
LANES = 128
F32 = jnp.float32
BF16 = jnp.bfloat16


def dot_nn(a, b):
    return lax.dot_general(a, b, (((1,), (0,)), ((), ())), preferred_element_type=F32)


def dot_nt(a, b):
    return lax.dot_general(a, b, (((1,), (1,)), ((), ())), preferred_element_type=F32)


def rotate_norm(first, second, cosine, sine, inv_dim):
    low = first * cosine - second * sine
    high = second * cosine + first * sine
    mean = jnp.sum(low * low + high * high, axis=0, keepdims=True) * inv_dim
    scale = lax.rsqrt(mean + NORM_EPS)
    return low * scale, high * scale, scale


def rotate_norm_pull(low, high, scale, cosine, sine, d_low, d_high, inv_dim, sm_scale):
    scale = scale * sm_scale
    mean = jnp.sum(low * d_low + high * d_high, axis=0, keepdims=True) * inv_dim
    r_low = (d_low - low * mean) * scale
    r_high = (d_high - high * mean) * scale
    return r_low * cosine + r_high * sine, r_high * cosine - r_low * sine


def block_kernel(sizes, ids_ref, table_ref, dh_ref, wqkv_ref, wqkv_t_ref, wo_ref, wo_t_ref, gain_ref, cos_ref, sin_ref,
                 h_ref, demb_ref, demb_tail_ref, gpack_ref,
                 gqkv_ref, gout_ref, ggain_ref, rows, stage, bias_ref, sems, xt, at, qkv, dmix, mixed, dqkv, dnorm):
    d_model, heads, kv_heads, head_dim, chunk, out_scale, share_rows, padded_rows, pack_columns, _ = sizes
    group = heads // kv_heads
    half = head_dim // 2
    inv_dim = 1.0 / head_dim
    seq_len = rows.shape[1]
    tiles = rows.shape[2]
    chunks = seq_len // chunk
    head_cols = demb_ref.shape[1]
    step = pl.program_id(0)
    last = pl.num_programs(0) - 1
    slot = lax.rem(step, 2)
    next_slot = 1 - slot
    next_base = jnp.minimum(step + 1, last) * seq_len

    def fetch(base, offset, into):
        pltpu.make_async_copy(table_ref.at[ids_ref[base + offset]], rows.at[into, offset], sems.at[into]).start()

    def wait_rows(which):
        pltpu.make_async_copy(table_ref.at[pl.ds(0, seq_len)], rows.at[which], sems.at[which]).wait()
    k_base = heads * head_dim
    v_base = k_base + kv_heads * head_dim
    row_blocks = [(r, min(LANES, d_model - r)) for r in range(0, d_model, LANES)]

    @pl.when(step == 0)
    def _():
        @pl.loop(0, seq_len)
        def _(t):
            fetch(0, t, 0)
        gqkv_ref[...] = jnp.zeros_like(gqkv_ref)
        gout_ref[...] = jnp.zeros_like(gout_ref)
        ggain_ref[...] = jnp.zeros_like(ggain_ref)

    def columns(w):
        return pl.ds(pl.multiple_of(w * chunk, chunk), chunk)

    dmix[...] = dot_nn(wo_ref[...], dh_ref[...]).astype(BF16)
    wait_rows(slot)

    @pl.loop(0, chunks)
    def _(w):
        cols = columns(w)
        stage[...] = rows[slot, cols].astype(F32).reshape(chunk * tiles, LANES)
        total = jnp.zeros((1, chunk), F32)
        for r, n in row_blocks:
            piece = stage[pl.ds(r // LANES, chunk, stride=tiles), :].T[:n]
            xt[r:r + n, cols] = piece
            total += jnp.sum(piece * piece, axis=0, keepdims=True)
        scale = lax.rsqrt(total * (1.0 / d_model) + NORM_EPS)
        for r, n in row_blocks:
            at[r:r + n, cols] = (xt[r:r + n, cols] * scale * gain_ref[r:r + n, :]).astype(BF16)

    qkv[...] = dot_nn(wqkv_t_ref[...], at[...])

    query_pos = lax.broadcasted_iota(jnp.int32, (chunk, chunk), 1)
    key_pos = lax.broadcasted_iota(jnp.int32, (chunk, chunk), 0)
    bias_ref[...] = jnp.where(query_pos >= key_pos, 0.0, -1e30)
    sm_scale = head_dim ** -0.5
    exp2_scale = sm_scale * LOG2_E

    @pl.loop(0, chunks)
    def _(w):
        cols = columns(w)
        cosine = cos_ref[:, cols]
        sine = sin_ref[:, cols]

        def rotated(base):
            return rotate_norm(qkv[base:base + half, cols], qkv[base + half:base + head_dim, cols], cosine, sine, inv_dim)

        everyone = range(kv_heads)
        bias = jnp.concatenate([bias_ref[...]] * group, axis=1)

        def fetch_share(part, parts):
            for t in range(chunk * part // parts, chunk * (part + 1) // parts):
                fetch(next_base, w * chunk + t, next_slot)

        key_parts = [rotated(k_base + kv * head_dim) for kv in everyone]
        key_f = [jnp.concatenate([lo, hi], axis=0) for lo, hi, _ in key_parts]
        key_t = [k.astype(BF16) for k in key_f]
        key = [k.T.astype(BF16) for k in key_f]
        value_f = [qkv[v_base + kv * head_dim:v_base + (kv + 1) * head_dim, cols] for kv in everyone]
        value_t = [v.astype(BF16) for v in value_f]
        value = [v.T.astype(BF16) for v in value_f]
        query_parts = [[rotated((kv * group + g) * head_dim) for g in range(group)] for kv in everyone]
        query_t = [jnp.concatenate([jnp.concatenate([lo, hi], axis=0).astype(BF16) for lo, hi, _ in parts], axis=1)
                   for parts in query_parts]
        dout_t = [jnp.concatenate(
            [dmix[(kv * group + g) * head_dim:(kv * group + g + 1) * head_dim, cols] for g in range(group)], axis=1)
            for kv in everyone]
        scores = [dot_nn(key[kv], query_t[kv]) for kv in everyone]
        d_probs = [dot_nn(value[kv], dout_t[kv]) for kv in everyone]
        weight = [jnp.exp2(scores[kv] * exp2_scale + bias) for kv in everyone]
        probs = [weight[kv] * (1.0 / jnp.sum(weight[kv], axis=0, keepdims=True)) for kv in everyone]
        probs_bf = [p.astype(BF16) for p in probs]
        fetch_share(0, 2)
        out_t = [dot_nn(value_t[kv], probs_bf[kv]).astype(BF16) for kv in everyone]
        d_value = [dot_nt(dout_t[kv], probs_bf[kv]) for kv in everyone]
        delta = [jnp.sum(probs[kv] * d_probs[kv], axis=0, keepdims=True) for kv in everyone]
        dscore_bf = [(probs[kv] * (d_probs[kv] - delta[kv])).astype(BF16) for kv in everyone]
        fetch_share(1, 2)
        d_query = [dot_nn(key_t[kv], dscore_bf[kv]) for kv in everyone]
        d_key = [dot_nt(query_t[kv], dscore_bf[kv]) for kv in everyone]
        for kv in everyone:
            kb = k_base + kv * head_dim
            vb = v_base + kv * head_dim
            for g in range(group):
                base = (kv * group + g) * head_dim
                lanes = slice(g * chunk, (g + 1) * chunk)
                mixed[base:base + head_dim, cols] = out_t[kv][:, lanes]
                lo, hi, scale = query_parts[kv][g]
                d_first, d_second = rotate_norm_pull(
                    lo, hi, scale, cosine, sine, d_query[kv][:half, lanes], d_query[kv][half:, lanes], inv_dim, sm_scale)
                dqkv[base:base + half, cols] = d_first.astype(BF16)
                dqkv[base + half:base + head_dim, cols] = d_second.astype(BF16)
            lo, hi, scale = key_parts[kv]
            d_first, d_second = rotate_norm_pull(
                lo, hi, scale, cosine, sine, d_key[kv][:half], d_key[kv][half:], inv_dim, sm_scale)
            dqkv[kb:kb + half, cols] = d_first.astype(BF16)
            dqkv[kb + half:kb + head_dim, cols] = d_second.astype(BF16)
            dqkv[vb:vb + head_dim, cols] = d_value[kv].astype(BF16)

    h_ref[...] = (xt[...] + dot_nn(wo_t_ref[...], mixed[...])).astype(BF16)
    dnorm[...] = dot_nn(wqkv_ref[...], dqkv[...])
    gout_ref[...] += dot_nt(mixed[...], dh_ref[...])
    gqkv_ref[...] += dot_nt(at[...], dqkv[...])

    @pl.loop(0, chunks, unroll=True)
    def _(w):
        cols = columns(w)
        total = jnp.zeros((1, chunk), F32)
        inner = jnp.zeros((1, chunk), F32)
        for r, n in row_blocks:
            piece = xt[r:r + n, cols]
            total += jnp.sum(piece * piece, axis=0, keepdims=True)
            inner += jnp.sum(piece * (dnorm[r:r + n, cols] * gain_ref[r:r + n, :]), axis=0, keepdims=True)
        scale = lax.rsqrt(total * (1.0 / d_model) + NORM_EPS)
        mean = inner * scale * (1.0 / d_model)
        for r, n in row_blocks:
            unit = xt[r:r + n, cols] * scale
            d_row = dnorm[r:r + n, cols]
            ggain_ref[r:r + n, :] += d_row * unit
            d_x = (d_row * gain_ref[r:r + n, :] - unit * mean) * scale
            full = (dh_ref[r:r + n, cols].astype(F32) + d_x) * out_scale
            if r < head_cols:
                demb_ref[cols, r:r + n] = full.T
            else:
                demb_tail_ref[cols, r - head_cols:r - head_cols + n] = full.T

    @pl.when(step == last)
    def _():
        wait_rows(next_slot)
        gpack_ref[...] = jnp.zeros_like(gpack_ref)

        @pl.loop(0, d_model // (2 * share_rows))
        def _(pair):
            source = pl.ds(pl.multiple_of(pair * 2 * share_rows, 8), 2 * share_rows)
            for grad, column in zip((ggain_ref, gqkv_ref, gout_ref), pack_columns):
                both = grad[source, :]
                for side in range(2):
                    target = pl.ds(pl.multiple_of((2 * pair + side) * padded_rows, 8), share_rows)
                    gpack_ref[target, column:column + grad.shape[1]] = both[side * share_rows:(side + 1) * share_rows]


def fused_block(ids, table, dh_t, wqkv, wqkv_t, wo, wo_t, gain_rows, cos_t, sin_t, sizes, head_cols, interpret=False):
    batch, d_model, seq_len = dh_t.shape
    tokens = batch * seq_len
    tiles = table.shape[1]
    width = wqkv.shape[1]
    mixed_width = wo.shape[0]
    pack_shape = (d_model // sizes[6] * sizes[7], sizes[9])

    def whole(shape):
        return pl.BlockSpec(shape, lambda b, ids: (0,) * len(shape), pipeline_mode=pl.Buffered(buffer_count=1))

    per_token = 2 * (3 * d_model * width + 3 * d_model * mixed_width) + 12 * mixed_width * sizes[4]
    return pl.pallas_call(
        functools.partial(block_kernel, sizes),
        grid_spec=pltpu.PrefetchScalarGridSpec(
            num_scalar_prefetch=1,
            grid=(batch,),
            in_specs=[
                pl.BlockSpec(memory_space=pl.ANY),
                pl.BlockSpec((None, d_model, seq_len), lambda b, ids: (b, 0, 0)),
                whole(wqkv.shape), whole(wqkv_t.shape), whole(wo.shape), whole(wo_t.shape),
                whole(gain_rows.shape), whole(cos_t.shape), whole(sin_t.shape),
            ],
            out_specs=[
                pl.BlockSpec((None, d_model, seq_len), lambda b, ids: (b, 0, 0)),
                pl.BlockSpec((seq_len, head_cols), lambda b, ids: (b, 0)),
                pl.BlockSpec((seq_len, d_model - head_cols), lambda b, ids: (b, 0)),
                whole(pack_shape),
            ],
            scratch_shapes=[
                pltpu.VMEM((d_model, width), F32),
                pltpu.VMEM((mixed_width, d_model), F32),
                pltpu.VMEM((d_model, sizes[4]), F32),
                pltpu.VMEM((2, seq_len, tiles, LANES), BF16),
                pltpu.VMEM((sizes[4] * tiles, LANES), F32),
                pltpu.VMEM((sizes[4], sizes[4]), F32),
                pltpu.SemaphoreType.DMA((2,)),
                pltpu.VMEM((d_model, seq_len), F32),
                pltpu.VMEM((d_model, seq_len), BF16),
                pltpu.VMEM((width, seq_len), F32),
                pltpu.VMEM((mixed_width, seq_len), BF16),
                pltpu.VMEM((mixed_width, seq_len), BF16),
                pltpu.VMEM((width, seq_len), BF16),
                pltpu.VMEM((d_model, seq_len), F32),
            ],
        ),
        out_shape=[
            jax.ShapeDtypeStruct(dh_t.shape, BF16),
            jax.ShapeDtypeStruct((tokens, head_cols), F32),
            jax.ShapeDtypeStruct((tokens, d_model - head_cols), F32),
            jax.ShapeDtypeStruct(pack_shape, F32),
        ],
        compiler_params=pltpu.CompilerParams(dimension_semantics=("arbitrary",), vmem_limit_bytes=60 * 1024 * 1024),
        cost_estimate=pl.CostEstimate(flops=per_token * tokens, bytes_accessed=tokens * d_model * 10, transcendentals=0),
        name="block",
        interpret=interpret,
    )(ids, table, dh_t, wqkv, wqkv_t, wo, wo_t, gain_rows, cos_t, sin_t)


def rotary_tables(seq_len, head_dim):
    half = head_dim // 2
    frequency = ROPE_THETA ** (-2.0 * jnp.arange(half, dtype=F32) / head_dim)
    angles = frequency[:, None] * jnp.arange(seq_len, dtype=F32)[None, :]
    return jnp.cos(angles), jnp.sin(angles)


def solution(mesh):
    group_count = mesh.shape['fsdp']

    def device_step(token_ids, embed_table, norm_gain, w_query, w_key, w_value, w_out, grad_out):
        batch, seq_len = token_ids.shape
        share, d_model = embed_table.shape
        heads, head_dim = w_query.shape[1:]
        kv_heads = w_key.shape[1]
        rows = w_query.shape[0]
        q_width, kv_width = heads * head_dim, kv_heads * head_dim
        width = q_width + 2 * kv_width

        packed = jnp.concatenate([
            w_query.reshape(rows, q_width), w_key.reshape(rows, kv_width), w_value.reshape(rows, kv_width),
            w_out, jnp.broadcast_to(norm_gain[:, None], (rows, LANES))], axis=1)
        weights = lax.all_gather(packed, 'fsdp', axis=0, tiled=True)
        tiles = 8 * pl.cdiv(d_model, 8 * LANES)
        row_tiles = jnp.pad(embed_table, ((0, 0), (0, tiles * LANES - d_model))).reshape(share, tiles, LANES)
        full_table = lax.all_gather(row_tiles, 'fsdp', axis=0, tiled=True)
        wqkv = weights[:, :width]
        wo = weights[:, width:width + d_model]
        gain_rows = weights[:, width + d_model:].astype(F32)
        cos_t, sin_t = rotary_tables(seq_len, head_dim)

        flat_ids = token_ids.reshape(-1)
        head_cols = (d_model // LANES + 1) // 2 * LANES
        chunk = seq_len // CHUNK_COUNT
        qkv_at = LANES
        out_at = qkv_at + pl.cdiv(width, LANES) * LANES
        pack_width = out_at + pl.cdiv(d_model, LANES) * LANES
        padded_rows = pl.cdiv(rows, 8) * 8
        sizes = (d_model, heads, kv_heads, head_dim, chunk, 1.0 / group_count, rows, padded_rows, (0, qkv_at, out_at), pack_width)
        h_t, d_head, d_tail, packed_grads = fused_block(
            flat_ids, full_table, jnp.swapaxes(grad_out, 1, 2), wqkv, wqkv.T, wo, wo.T, gain_rows, cos_t, sin_t, sizes, head_cols)

        grads = lax.psum_scatter(packed_grads, 'fsdp', scatter_dimension=0, tiled=True)[:rows] / group_count
        g_gain = jnp.sum(grads[:, :chunk], axis=1)
        g_qkv = grads[:, qkv_at:qkv_at + width]
        g_out = grads[:, out_at:out_at + d_model]

        def table_share(rows_grad):
            total = jnp.zeros((share * group_count, rows_grad.shape[1]), F32)
            total = total.at[flat_ids].add(rows_grad, mode='promise_in_bounds')
            return lax.psum_scatter(total, 'fsdp', scatter_dimension=0, tiled=True)

        table_grad = jnp.concatenate([table_share(d_head).T, table_share(d_tail).T], axis=0).T
        return (jnp.swapaxes(h_t, 1, 2), table_grad, g_gain,
                g_qkv[:, :q_width].reshape(w_query.shape),
                g_qkv[:, q_width:q_width + kv_width].reshape(w_key.shape),
                g_qkv[:, q_width + kv_width:].reshape(w_value.shape), g_out)

    tokens = P('fsdp', None, None)
    matrix = P('fsdp', None)
    vector = P('fsdp')
    return jax.shard_map(device_step, mesh=mesh, in_specs=(matrix, matrix, vector, tokens, tokens, tokens, matrix, tokens), out_specs=(tokens, matrix, vector, tokens, tokens, tokens, matrix), check_vma=False)
```

time: 3830 us -> 2170 us (0.57)
  matrix products: 1130 us -> 0 us
  local copies, waits for them, and re-layouts: 887 us -> 60.3 us
  Pallas kernels: 0 us -> 527 us
  other arithmetic: 802 us -> 529 us
  waiting for transfers between devices: 817 us -> 1030 us
  blocking collectives: 152 us -> 0 us
    dot_general x18 -> x0, matrix products: 1130 us -> none  [the longest x1 195 us: block_backward(): jnp.einsum('bckigj,bcjkd->bcikgd', dscore_bf, saved['key_bf'], preferred_...]
    reduce_scatter x0 -> x3, waiting for transfers between devices: none -> 675 us  [the longest x2 675 us: table_share(): return lax.psum_scatter(total, 'fsdp', scatter_dimension=0, tiled=True)]
    unnamed x8 -> x5, waiting for transfers between devices: 581 us -> 0.08 us
    pallas_call x0 -> x1, Pallas kernels: none -> 527 us  [fused_block(): pl.pallas_call(functools.partial(block_kernel, sizes), grid_spec=pltpu.Pr...]
    gather x2 -> x0, local copies, waits for them, and re-layouts: 343 us -> none  [device_step(): embedded = jnp.take(full_table, token_ids, axis=0)]
    reshape x5, local copies, waits for them, and re-layouts: 242 us -> 11.3 us  [the longest x1 8.95 us: device_step(): jnp.pad(embed_table, ((0, 0), (0, tiles * LANES - d_model)))]
    scatter-add x3 -> x4, other arithmetic: 370 us -> 513 us  [table_share(): total = total.at[flat_ids].add(rows_grad, mode='promise_in_bounds')]
    add_any x4 -> x0, other arithmetic: 131 us -> none  [the longest x2 81.9 us: rms_scale(): values * values]
  transfers between devices with their start and end apart: 6 -> 5, of which waited for: 2 -> 4; matrix products, arithmetic and copies ran while one was open for 24% -> 26% of each run, Pallas kernels for 0% -> 0%
where the time goes in v1:
time: 2170 us; the launch traced here: 2160 us
  waiting for transfers between devices  1030 us (47%)
  other arithmetic  529 us (24%)
  Pallas kernels  527 us (24%)
  local copies, waits for them, and re-layouts  60.3 us (3%)
    reduce_scatter x2, waiting for transfers between devices, table_share(): return lax.psum_scatter(total, 'fsdp', scatter_dimension=0, tiled=True)  675 us
    pallas_call x1, Pallas kernels, fused_block(): pl.pallas_call(functools.partial(block_kernel, sizes), grid_spec=pltpu.Pr...  527 us
    scatter-add x4, other arithmetic, table_share(): total = total.at[flat_ids].add(rows_grad, mode='promise_in_bounds')  513 us
    all_gather x1, waiting for transfers between devices, device_step(): full_table = lax.all_gather(row_tiles, 'fsdp', axis=0, tiled=True)  330 us
  transfers between devices with their start and end apart: 5, of which 4 were waited for; matrix products, arithmetic and copies ran while one was open for 26% of the time, Pallas kernels for 0%

profile of v1, /device:TPU:0, one launch (start us, length us, event | category | flops | bytes accessed | tf_op | source)
XLA Modules:
  0.0 2161.3 jit_solution(15706796633969190163)
XLA Ops:
  7.2 1.0 copy.37
  8.3 1.0 copy.38
  9.5 1.1 reshape.76
  11.4 1.8 concatenate.6
  13.3 5.9 pad.4
  19.1 9.0 copy.50
  28.2 1.5 copy.53
  30.6 24.8 %all-gather.6.cloned.1.call-done = bf16[16,60,2688]{2,1,0:T(8,128)(2,1)} async-done(((bf16[1,60,2688]{2,1,0:T(8,128)(2,1)}), bf16[16,60,2688]{2,1,0:T(8,128)(2,1)}) %all-gather.6.cloned.1.call-update) | async-done | bytes 5160976 | tf_op jit(solution)/shard_map/all_gather | solution.py:289
  55.4 7.5 reshape.100
  62.9 2.1 slice.44.wqkv_ref
  65.1 5.0 slice.45.wo_ref
  70.1 3.6 copy.51
  73.6 3.8 copy.52
  77.5 1.8 slice_convert_fusion.gain_ref
  79.2 330.3 %all-gather.4.cloned.1.call-done.table_ref = bf16[49152,8,128]{2,1,0:T(8,128)(2,1)} async-done(((bf16[3072,8,128]{2,1,0:T(8,128)(2,1)}), bf16[49152,8,128]{2,1,0:T(8,128)(2,1)}) %all-gather.4.cloned.1.call-update) | async-done | bytes 100663312 | tf_op jit(solution)/shard_map/all_gather | solution.py:292
  409.5 527.3 %block.1 = (bf16[32,960,512]{2,1,0:T(8,128)(2,1)}, f32[16384,512]{1,0:T(8,128)}, f32[16384,448]{1,0:T(8,128)}, f32[1024,2816]{1,0:T(8,128)}) custom-call(s32[16384]{0:T(1024)} %bitcast.35, bf16[49152,8,128]{2,1,0:T(8,128)(2,1)} %all-gather.4.cloned.1.call-done.table_ref, bf16[32,960,512]{2,1,0:T(8,128)(2,1)} %bitcast.36, bf16[960,1600]{1,0:T(8,128)(2,1)} %copy-done, ...), custom_call_target="tpu_custom_call" | custom-call | flops 265751101440 | bytes 157286400 | tf_op jit(solution)/shard_map/block/pallas_call | solution.py:220
  937.6 7.1 sort
  944.8 252.8 %scatter_custom_fusion.1 = f32[49152,448]{1,0:T(8,128)} fusion(s32[16384]{0:T(1024)S(1)} %get-tuple-element.36, f32[]{:T(128)} %constant.4.clone.1, f32[16384,448]{1,0:T(8,128)} %get-tuple-element.13, s32[16384]{0:T(1024)S(1)} %broadcast_clamp_fusion), kind=kCustom, calls=%fused_computation.4 | custom fusion | flops 7340032 | bytes 88080896 | tf_op jit(solution)/shard_map/scatter-add | solution.py:316
  1197.6 252.6 %scatter_custom_fusion = f32[49152,512]{1,0:T(8,128)} fusion(s32[16384]{0:T(1024)S(1)} %get-tuple-element.36, f32[]{:T(128)} %constant.4.clone.1, f32[16384,512]{1,0:T(8,128)} %get-tuple-element.12, s32[16384]{0:T(1024)S(1)} %broadcast_clamp_fusion), kind=kCustom, calls=%fused_computation.6 | custom fusion | flops 8388608 | bytes 100663808 | tf_op jit(solution)/shard_map/scatter-add | solution.py:316
  1450.3 1.2 slice_multiply_fusion
  1455.7 206.0 %reduce-scatter.6.cloned.1.call-done = f32[3072,448]{1,0:T(8,128)} async-done(((f32[49152,448]{1,0:T(8,128)}), f32[3072,448]{1,0:T(8,128)}) %reduce-scatter.6.cloned.1.call-update) | async-done | bytes 5505040 | tf_op jit(solution)/shard_map/reduce_scatter | solution.py:317
  1661.7 468.7 %reduce-scatter.4.cloned.1.call-done = f32[3072,512]{1,0:T(8,128)} async-done(((f32[49152,512]{1,0:T(8,128)}), f32[3072,512]{1,0:T(8,128)}) %reduce-scatter.4.cloned.1.call-update) | async-done | bytes 6291472 | tf_op jit(solution)/shard_map/reduce_scatter | solution.py:317
  2130.4 11.6 maximum_bitcast_fusion
  2142.0 12.3 copy.47
  (32 shorter events, 7.1 us)
Async XLA Ops:
  7.2 48.2 %all-gather.6.cloned.1.call-start = ((), (), s32[]{:S(2)}) async-start(), calls=%async_computation.7 | async-start | bytes 5849088 | tf_op jit(solution)/shard_map/all_gather | solution.py:289
  13.2 396.3 %all-gather.4.cloned.1.call-start = ((), (), s32[]{:S(2)}) async-start(), calls=%async_computation.3 | async-start | bytes 106954752 | tf_op jit(solution)/shard_map/all_gather | solution.py:292
  28.1 1422.1 %reduce-scatter.8.cloned.1.call-start = ((), (), s32[]{:S(2)}) async-start(), calls=%async_computation.6 | async-start | bytes 12255232 | tf_op jit(solution)/shard_map/reduce_scatter | solution.py:309
  65.1 344.5 %copy-start = (bf16[960,1600]{1,0:T(8,128)(2,1)}, bf16[960,1600]{1,0:T(8,128)(2,1)S(1)}, u32[]{:S(2)}) copy-start(bf16[960,1600]{1,0:T(8,128)(2,1)S(1)} %slice.44.wqkv_ref) | copy-start | bytes 9216004
  409.5 527.9 %copy-start.1 = (s32[32,512]{1,0:T(8,128)S(1)}, s32[32,512]{1,0:T(8,128)}, u32[]{:S(2)}) copy-start(s32[32,512]{1,0:T(8,128)} %param.8) | copy-start | bytes 196612
  936.9 724.8 %reduce-scatter.6.cloned.1.call-start = ((), (), s32[]{:S(2)}) async-start(), calls=%async_computation.5 | async-start | bytes 106954752 | tf_op jit(solution)/shard_map/reduce_scatter | solution.py:317
  1197.6 932.9 %reduce-scatter.4.cloned.1.call-start = ((), (), s32[]{:S(2)}) async-start(), calls=%async_computation.4 | async-start | bytes 106954752 | tf_op jit(solution)/shard_map/reduce_scatter | solution.py:317
Sparse Core Ops, SparseCore 0:
  13.3 42.0 all-gather.5
  58.2 351.2 all-gather.3
  937.0 124.4 reduce-scatter.7
  1197.7 463.9 reduce-scatter.5
  1666.5 463.9 reduce-scatter.3
